TPU v7x, 32 devices: a whole 2x2x4 slice. The times are simulated.
32 devices in a mesh: tm: 4 (over y, x), rows: 2 (over core), batch: 4 (over z).
Axes of the slice: x: 2, y: 2, z: 4, core: 2. Of those that a mesh axis runs over, the one named last changes fastest.
Arguments:
- inputs: bfloat16 [4, 8, 16, 128, 384], P('batch', 'tm', 'rows'), parts along dimension 0, may hold values from -16 to 16
- norm_gain: float32 [384], replicated, may hold values from 0.1 to 1.9
- norm_bias: float32 [384], replicated, may hold values from -3 to 3
- conv_weight: bfloat16 [3, 3, 3, 384, 384], replicated, may hold values from -0.0625 to 0.0625
- conv_bias: float32 [384], replicated, may hold values from -2 to 2
Outputs:
- decoded: bfloat16 [4, 8, 16, 128, 384], P('batch', 'tm', 'rows'), parts along dimension 0
There are 4 independent parts, one for each index of `batch`. A program takes and returns all parts, laid end to end along the dimension named above; an argument that names none is the same for every part. Nothing has to cross between parts.
All inputs are finite; a program needn't handle non-finite values.
Results may differ from a plain program's by a relative error of at most 0.0025.
Values may be sent and summed in bfloat16 or wider, within the bound.
A program may use at most 128 MiB of HBM per device.

v0:
```python
import functools

import jax
import jax.numpy as jnp
from jax import lax
from jax.experimental import pallas as pl
from jax.experimental.pallas import tpu as pltpu
from jax.sharding import PartitionSpec as P

GROUPS = 32
MESH = pl.DeviceIdType.MESH
OWN_ROWS = 4
EARLY = 2

epsilon = 1e-06


def block_kernel(
    T, R, x_hbm, gain_hbm, nbias_hbm, w_hbm, cbias_hbm, out_ref,
    params, p_sem, xv, wv, hraw, eown, ehalo, own3, halo3, edge3, acc, stats,
    x_sem, w_sem, halo_send, halo_recv, eown_send, eown_recv,
    ehalo_send, ehalo_recv, stat_send, stat_recv,
):
    F, H, W, C = x_hbm.shape
    C3 = 3 * C
    n = T * R
    tm = lax.axis_index("tm")
    row = lax.axis_index("rows")
    me = tm * R + row

    def peer(offset):
        other = lax.rem(me + offset, n)
        return {"tm": other // R, "rows": lax.rem(other, R)}

    x_copies = [pltpu.make_async_copy(x_hbm.at[f], xv.at[f], x_sem.at[f]) for f in range(F)]
    w_copies = [
        pltpu.make_async_copy(
            w_hbm.at[kt, kh], wv.at[kt, :, pl.ds(kh * C, C)], w_sem.at[kt * 3 + kh]
        )
        for kt in range(3)
        for kh in range(3)
    ]
    p_copies = [
        pltpu.make_async_copy(p, params.at[k, 0], p_sem.at[k])
        for k, p in enumerate((gain_hbm, nbias_hbm, cbias_hbm))
    ]
    barrier = pltpu.get_barrier_semaphore()
    for d in range(1, n):
        pl.semaphore_signal(barrier, inc=1, device_id=peer(d), device_id_type=MESH)
    for c in x_copies + p_copies:
        c.start()
    pl.semaphore_wait(barrier, n - 1)

    def row_of(i):
        return jnp.where(i == 0, 0, jnp.where(i == 1, H - 1, i - 1))

    def halo_copy(i, r):
        return pltpu.make_async_remote_copy(
            src_ref=x_hbm.at[pl.ds(F - 2, 2), pl.ds(r, 1)],
            dst_ref=hraw.at[:, pl.ds(r, 1)],
            send_sem=halo_send.at[i],
            recv_sem=halo_recv.at[i],
            device_id={"tm": lax.rem(tm + 1, T), "rows": row},
            device_id_type=MESH,
        )

    def own_edge(side):
        r = H - 1 if side == 0 else 0
        target = row + 1 if side == 0 else row - 1
        return pltpu.make_async_remote_copy(
            src_ref=x_hbm.at[:, pl.ds(r, 1)],
            dst_ref=eown.at[side],
            send_sem=eown_send.at[side],
            recv_sem=eown_recv.at[side],
            device_id={"tm": tm, "rows": lax.rem(target + R, R)},
            device_id_type=MESH,
        )

    def halo_edge(side):
        r = H - 1 if side == 0 else 0
        target = row + 1 if side == 0 else row - 1
        return pltpu.make_async_remote_copy(
            src_ref=hraw.at[:, pl.ds(r, 1)],
            dst_ref=ehalo.at[side],
            send_sem=ehalo_send.at[side],
            recv_sem=ehalo_recv.at[side],
            device_id={"tm": tm, "rows": lax.rem(target + R, R)},
            device_id_type=MESH,
        )

    has_next, has_prev = tm < T - 1, tm > 0
    sends_edge = (row < R - 1, row > 0)
    gets_edge = (row > 0, row < R - 1)

    @pl.when(has_next)
    def _():
        for i in range(EARLY):
            halo_copy(i, 0 if i == 0 else H - 1 if i == 1 else i - 1).start()

    for side in range(2):
        @pl.when(sends_edge[side])
        def _():
            own_edge(side).start()

    for c in w_copies:
        c.start()

    total = jnp.zeros((8, C), jnp.float32)
    square = jnp.zeros((8, C), jnp.float32)
    for f in range(F):
        x_copies[f].wait()

        def add_rows(r, carry):
            v = xv[f, r].astype(jnp.float32).reshape(W // 8, 8, C)
            return carry[0] + jnp.sum(v, axis=0), carry[1] + jnp.sum(v * v, axis=0)

        total, square = lax.fori_loop(0, H, add_rows, (total, square))
    stats[0, 0:8] = total
    stats[0, 8:16] = square

    def stat_copy(d):
        return pltpu.make_async_remote_copy(
            src_ref=stats.at[0],
            dst_ref=stats.at[d],
            send_sem=stat_send.at[d],
            recv_sem=stat_recv.at[d],
            device_id=peer(d),
            device_id_type=MESH,
        )

    for d in range(1, n):
        stat_copy(d).start()

    @pl.when(has_next)
    def _():
        for i in range(EARLY, H):
            halo_copy(i, 0 if i == 0 else H - 1 if i == 1 else i - 1).start()

    for c in p_copies:
        c.wait()
    for f in range(F):
        def start_acc(r, _):
            acc[f, r + 1] = xv[f, r].astype(jnp.float32) + params[2]
            return 0

        lax.fori_loop(0, H, start_acc, 0)
    for d in range(1, n):
        stat_copy(d).wait_recv()
    total = stats[0]
    for d in range(1, n):
        total = total + stats[d]
    sums = jnp.concatenate(
        [
            jnp.broadcast_to(jnp.sum(total[0:8], axis=0, keepdims=True), (8, C)),
            jnp.broadcast_to(jnp.sum(total[8:16], axis=0, keepdims=True), (8, C)),
        ],
        axis=0,
    )
    per_group = C // GROUPS
    channel = lax.broadcasted_iota(jnp.int32, (C, C), 0)
    other = lax.broadcasted_iota(jnp.int32, (C, C), 1)
    first = (other // per_group) * per_group
    member = jnp.where((channel >= first) & (channel < first + per_group), 1.0, 0.0)
    cells = 1.0 * F * H * W * per_group * n
    moments = (
        jnp.dot(
            sums,
            member.astype(jnp.float32),
            preferred_element_type=jnp.float32,
            precision=lax.Precision.HIGHEST,
        )
        / cells
    )
    mean = moments[0:1]
    var = jnp.maximum(moments[8:9] - mean * mean, 0.0)
    half_scale = lax.rsqrt(var + epsilon) * params[0] * 0.5
    half_bias = params[1] * 0.5

    column = lax.broadcasted_iota(jnp.int32, (W, C), 0)

    def activate(raw, put):
        h = (raw.astype(jnp.float32) - mean) * half_scale + half_bias
        a = h + h * jnp.tanh(h)
        put(0, jnp.where(column == 0, 0.0, pltpu.roll(a, 1, 0)).astype(jnp.bfloat16))
        put(1, a.astype(jnp.bfloat16))
        put(2, jnp.where(column == W - 1, 0.0, pltpu.roll(a, W - 1, 0)).astype(jnp.bfloat16))

    for f in range(F):
        def own_row(r, _):
            def put(k, v):
                own3[f, r, :, k * C : (k + 1) * C] = v

            activate(xv[f, r], put)
            return 0

        lax.fori_loop(0, H, own_row, 0)

    @pl.when(has_prev)
    def _():
        for i in range(2):
            halo_copy(i, 0 if i == 0 else H - 1).wait_recv()
        for side in range(2):
            @pl.when(sends_edge[side])
            def _():
                halo_edge(side).start()

    for c in w_copies:
        c.wait()

    def product(lhs, kt, lo=0, hi=3):
        return jnp.dot(
            lhs, wv[kt, :, lo * C : hi * C], preferred_element_type=jnp.float32
        )

    def finish(r, _):
        for f in range(F):
            out_ref[f, r] = acc[f, r + 1].astype(out_ref.dtype)
        return 0

    def own_rows(g, _):
        r0 = g * OWN_ROWS
        for kt in range(3):
            count = F - 2 + kt
            if count <= 0:
                continue
            lhs = own3[0:count, pl.ds(r0, OWN_ROWS)].reshape(count * OWN_ROWS * W, C3)
            y = product(lhs, kt)
            for kh in range(3):
                part = y[:, kh * C : (kh + 1) * C].reshape(count, OWN_ROWS, W, C)
                acc[2 - kt : 2 - kt + count, pl.ds(r0 + 2 - kh, OWN_ROWS)] += part
        return 0

    lax.fori_loop(0, H // OWN_ROWS, own_rows, 0)

    for side in range(2):
        kh = 0 if side == 0 else 2
        at = 1 if side == 0 else H

        @pl.when(gets_edge[side])
        def _():
            own_edge(side).wait_recv()
            for f in range(F):
                def put(k, v):
                    edge3[f, :, k * C : (k + 1) * C] = v

                activate(eown[side, f, 0], put)
            for kt in range(3):
                count = F - 2 + kt
                if count > 0:
                    lhs = edge3[0:count].reshape(count * W, C3)
                    acc[2 - kt : 2 - kt + count, at] += product(lhs, kt, kh, kh + 1).reshape(
                        count, W, C
                    )

    @pl.when(has_prev)
    def _():
        def halo_row(i, _):
            r = row_of(i)

            @pl.when(i >= 2)
            def _():
                halo_copy(i, r).wait_recv()

            for f in range(2):
                def put(k, v):
                    halo3[f, :, k * C : (k + 1) * C] = v

                activate(hraw[f, r], put)
            y = product(halo3[...].reshape(2 * W, C3), 0)
            z = product(halo3[1], 1)
            for kh in range(3):
                cols = slice(kh * C, (kh + 1) * C)
                acc[0, r + 2 - kh] += y[:W, cols] + z[:, cols]
                acc[1, r + 2 - kh] += y[W:, cols]

            @pl.when(i >= 2)
            def _():
                finish(i - 2, 0)

            return 0

        lax.fori_loop(0, 2, halo_row, 0)
        for side in range(2):
            kh = 0 if side == 0 else 2
            at = 1 if side == 0 else H

            @pl.when(gets_edge[side])
            def _():
                halo_edge(side).wait_recv()
                for f in range(2):
                    def put(k, v):
                        halo3[f, :, k * C : (k + 1) * C] = v

                    activate(ehalo[side, f, 0], put)
                y = product(halo3[...].reshape(2 * W, C3), 0, kh, kh + 1)
                z = product(halo3[1], 1, kh, kh + 1)
                acc[0, at] += y[:W] + z
                acc[1, at] += y[W:]

        lax.fori_loop(2, H, halo_row, 0)
        lax.fori_loop(max(H - 2, 0), H, finish, 0)

    @pl.when(jnp.logical_not(has_prev))
    def _():
        lax.fori_loop(0, H, finish, 0)

    for d in range(1, n):
        stat_copy(d).wait_send()

    @pl.when(has_next)
    def _():
        for i in range(H):
            halo_copy(i, 0 if i == 0 else H - 1 if i == 1 else i - 1).wait_send()

    for side in range(2):
        @pl.when(sends_edge[side])
        def _():
            own_edge(side).wait_send()

            @pl.when(has_prev)
            def _():
                halo_edge(side).wait_send()


def shards(T, R, inputs, norm_gain, norm_bias, conv_weight, conv_bias):
    _, F, H, W, C = inputs.shape
    n = T * R

    def pin(a):
        return pltpu.with_memory_space_constraint(a, pltpu.HBM)

    vmem = pl.BlockSpec(memory_space=pltpu.VMEM)
    hbm = pl.BlockSpec(memory_space=pltpu.HBM)
    anywhere = pl.BlockSpec(memory_space=pl.ANY)
    dma = pltpu.SemaphoreType.DMA
    out = pl.pallas_call(
        functools.partial(block_kernel, T, R),
        out_shape=jax.ShapeDtypeStruct((F, H, W, C), inputs.dtype),
        in_specs=[hbm, anywhere, anywhere, hbm, anywhere],
        out_specs=vmem,
        scratch_shapes=[
            pltpu.VMEM((3, 1, C), jnp.float32),
            dma((3,)),
            pltpu.VMEM((F, H, W, C), jnp.bfloat16),
            pltpu.VMEM((3, 3 * C, 3 * C), jnp.bfloat16),
            pltpu.VMEM((2, H, W, C), jnp.bfloat16),
            pltpu.VMEM((2, F, 1, W, C), jnp.bfloat16),
            pltpu.VMEM((2, 2, 1, W, C), jnp.bfloat16),
            pltpu.VMEM((F, H, W, 3 * C), jnp.bfloat16),
            pltpu.VMEM((2, W, 3 * C), jnp.bfloat16),
            pltpu.VMEM((F, W, 3 * C), jnp.bfloat16),
            pltpu.VMEM((F, H + 2, W, C), jnp.float32),
            pltpu.VMEM((n, 16, C), jnp.float32),
            dma((F,)),
            dma((9,)),
            dma((H,)),
            dma((H,)),
            dma((2,)),
            dma((2,)),
            dma((2,)),
            dma((2,)),
            dma((n,)),
            dma((n,)),
        ],
        compiler_params=pltpu.CompilerParams(
            collective_id=0, has_side_effects=True, vmem_limit_bytes=50 * 1024 * 1024
        ),
        name="norm_conv_block",
    )(
        pin(inputs.reshape(F, H, W, C)),
        pin(norm_gain),
        pin(norm_bias),
        pin(conv_weight.reshape(3, 3, 3 * C, C)),
        pin(conv_bias),
    )
    return out.reshape(inputs.shape)


def solution(mesh):
    placed = (P("batch", "tm", "rows", None, None), P(), P(), P(), P())
    return jax.shard_map(
        functools.partial(shards, mesh.shape["tm"], mesh.shape["rows"]),
        mesh=mesh,
        in_specs=placed,
        out_specs=P("batch", "tm", "rows", None, None),
        check_vma=False,
    )
```

profile of v0, /device:TPU:10, one launch (start us, length us, event | category | flops | bytes accessed | tf_op | source)
XLA Modules:
  0.0 43.2 jit_solution(18122671532430666689)
XLA Ops:
  0.0 42.0 %norm_conv_block.1 = bf16[2,8,128,384]{3,2,1,0:T(8,128)(2,1)S(1)} custom-call(bf16[2,8,128,384]{3,2,1,0:T(8,128)(2,1)} %bitcast.5, f32[384]{0:T(512)} %gain_hbm.1, f32[384]{0:T(512)} %nbias_hbm.1, bf16[3,3,1152,384]{3,2,1,0:T(8,128)(2,1)} %bitcast.4, f32[384]{0:T(512)} %cbias_hbm.1), custom_call_target="tpu_custom_call" | custom-call | tf_op jit(solution)/shard_map/norm_conv_block/pallas_call | solution.py:336
  42.0 1.1 %copy.7 = bf16[1,2,8,128,384]{4,3,2,1,0:T(8,128)(2,1)} copy(bf16[1,2,8,128,384]{4,3,2,1,0:T(8,128)(2,1)S(1)} %bitcast.3) | data formatting | bytes 3145728
where the time goes:
time: 43.3 us; the launch traced here: 43.2 us
  Pallas kernels  42 us (97%)
  local copies, waits for them, and re-layouts  1.15 us (3%)
    pallas_call x1, Pallas kernels, shards(): pl.pallas_call(functools.partial(block_kernel, T, R), out_shape=jax.Shape...  42 us
    unnamed x1, local copies, waits for them, and re-layouts  1.15 us

commit v1 on v0

--- a/solution.py
+++ b/solution.py
@@ -10,7 +10,6 @@
 GROUPS = 32
 MESH = pl.DeviceIdType.MESH
 OWN_ROWS = 4
-EARLY = 2
 
 epsilon = 1e-06
 
@@ -49,14 +48,12 @@
         pl.semaphore_signal(barrier, inc=1, device_id=peer(d), device_id_type=MESH)
     for c in x_copies + p_copies:
         c.start()
-    pl.semaphore_wait(barrier, n - 1)
-
     def row_of(i):
         return jnp.where(i == 0, 0, jnp.where(i == 1, H - 1, i - 1))
 
     def halo_copy(i, r):
         return pltpu.make_async_remote_copy(
-            src_ref=x_hbm.at[pl.ds(F - 2, 2), pl.ds(r, 1)],
+            src_ref=xv.at[pl.ds(F - 2, 2), pl.ds(r, 1)],
             dst_ref=hraw.at[:, pl.ds(r, 1)],
             send_sem=halo_send.at[i],
             recv_sem=halo_recv.at[i],
@@ -64,11 +61,21 @@
             device_id_type=MESH,
         )
 
+    def last_copy(f):
+        return pltpu.make_async_remote_copy(
+            src_ref=xv.at[F - 2 + f, H - 2],
+            dst_ref=hraw.at[f, H - 2],
+            send_sem=halo_send.at[H - 1 + f],
+            recv_sem=halo_recv.at[H - 1 + f],
+            device_id={"tm": lax.rem(tm + 1, T), "rows": row},
+            device_id_type=MESH,
+        )
+
     def own_edge(side):
         r = H - 1 if side == 0 else 0
         target = row + 1 if side == 0 else row - 1
         return pltpu.make_async_remote_copy(
-            src_ref=x_hbm.at[:, pl.ds(r, 1)],
+            src_ref=xv.at[:, pl.ds(r, 1)],
             dst_ref=eown.at[side],
             send_sem=eown_send.at[side],
             recv_sem=eown_recv.at[side],
@@ -92,16 +99,6 @@
     sends_edge = (row < R - 1, row > 0)
     gets_edge = (row > 0, row < R - 1)
 
-    @pl.when(has_next)
-    def _():
-        for i in range(EARLY):
-            halo_copy(i, 0 if i == 0 else H - 1 if i == 1 else i - 1).start()
-
-    for side in range(2):
-        @pl.when(sends_edge[side])
-        def _():
-            own_edge(side).start()
-
     for c in w_copies:
         c.start()
 
@@ -115,8 +112,9 @@
             return carry[0] + jnp.sum(v, axis=0), carry[1] + jnp.sum(v * v, axis=0)
 
         total, square = lax.fori_loop(0, H, add_rows, (total, square))
-    stats[0, 0:8] = total
-    stats[0, 8:16] = square
+    stats[0, 0:1] = jnp.sum(total, axis=0, keepdims=True)
+    stats[0, 1:2] = jnp.sum(square, axis=0, keepdims=True)
+    pl.semaphore_wait(barrier, n - 1)
 
     def stat_copy(d):
         return pltpu.make_async_remote_copy(
@@ -133,8 +131,15 @@
 
     @pl.when(has_next)
     def _():
-        for i in range(EARLY, H):
+        for i in range(H - 1):
             halo_copy(i, 0 if i == 0 else H - 1 if i == 1 else i - 1).start()
+        for f in (1, 0):
+            last_copy(f).start()
+
+    for side in range(2):
+        @pl.when(sends_edge[side])
+        def _():
+            own_edge(side).start()
 
     for c in p_copies:
         c.wait()
@@ -151,8 +156,8 @@
         total = total + stats[d]
     sums = jnp.concatenate(
         [
-            jnp.broadcast_to(jnp.sum(total[0:8], axis=0, keepdims=True), (8, C)),
-            jnp.broadcast_to(jnp.sum(total[8:16], axis=0, keepdims=True), (8, C)),
+            jnp.broadcast_to(total[0:1], (8, C)),
+            jnp.broadcast_to(total[1:2], (8, C)),
         ],
         axis=0,
     )
@@ -297,8 +302,25 @@
                 acc[0, at] += y[:W] + z
                 acc[1, at] += y[W:]
 
-        lax.fori_loop(2, H, halo_row, 0)
-        lax.fori_loop(max(H - 2, 0), H, finish, 0)
+        lax.fori_loop(2, H - 1, halo_row, 0)
+
+        r = H - 2
+        for f in (1, 0):
+            last_copy(f).wait_recv()
+
+            def put(k, v):
+                halo3[f, :, k * C : (k + 1) * C] = v
+
+            activate(hraw[f, r], put)
+            y = product(halo3[f], 0)
+            if f == 1:
+                z = product(halo3[f], 1)
+                for kh in range(3):
+                    acc[0, r + 2 - kh] += z[:, kh * C : (kh + 1) * C]
+            for kh in range(3):
+                out_ref[f, r + 1 - kh] = (
+                    acc[f, r + 2 - kh] + y[:, kh * C : (kh + 1) * C]
+                ).astype(out_ref.dtype)
 
     @pl.when(jnp.logical_not(has_prev))
     def _():
@@ -309,8 +331,10 @@
 
     @pl.when(has_next)
     def _():
-        for i in range(H):
+        for i in range(H - 1):
             halo_copy(i, 0 if i == 0 else H - 1 if i == 1 else i - 1).wait_send()
+        for f in (1, 0):
+            last_copy(f).wait_send()
 
     for side in range(2):
         @pl.when(sends_edge[side])
@@ -350,11 +374,11 @@
             pltpu.VMEM((2, W, 3 * C), jnp.bfloat16),
             pltpu.VMEM((F, W, 3 * C), jnp.bfloat16),
             pltpu.VMEM((F, H + 2, W, C), jnp.float32),
-            pltpu.VMEM((n, 16, C), jnp.float32),
+            pltpu.VMEM((n, 2, C), jnp.float32),
             dma((F,)),
             dma((9,)),
-            dma((H,)),
-            dma((H,)),
+            dma((H + 1,)),
+            dma((H + 1,)),
             dma((2,)),
             dma((2,)),
             dma((2,)),

time: 43.3 us -> 42.2 us (0.975)
  the two profiles are of different devices: /device:TPU:10 before, /device:TPU:4 now
where the time goes in v1:
time: 42.2 us; the launch traced here: 42.1 us
  Pallas kernels  40.9 us (97%)
  local copies, waits for them, and re-layouts  1.15 us (3%)
    pallas_call x1, Pallas kernels, shards(): pl.pallas_call(functools.partial(block_kernel, T, R), out_shape=jax.Shape...  40.9 us
    unnamed x1, local copies, waits for them, and re-layouts  1.15 us

profile of v1, /device:TPU:4, one launch (start us, length us, event | category | flops | bytes accessed | tf_op | source)
XLA Modules:
  0.0 42.1 jit_solution(4823240000619681088)
XLA Ops:
  0.0 40.9 %norm_conv_block.1 = bf16[2,8,128,384]{3,2,1,0:T(8,128)(2,1)S(1)} custom-call(bf16[2,8,128,384]{3,2,1,0:T(8,128)(2,1)} %bitcast.5, f32[384]{0:T(512)} %gain_hbm.1, f32[384]{0:T(512)} %nbias_hbm.1, bf16[3,3,1152,384]{3,2,1,0:T(8,128)(2,1)} %bitcast.4, f32[384]{0:T(512)} %cbias_hbm.1), custom_call_target="tpu_custom_call" | custom-call | tf_op jit(solution)/shard_map/norm_conv_block/pallas_call | solution.py:360
  40.9 1.1 %copy.7 = bf16[1,2,8,128,384]{4,3,2,1,0:T(8,128)(2,1)} copy(bf16[1,2,8,128,384]{4,3,2,1,0:T(8,128)(2,1)S(1)} %bitcast.3) | data formatting | bytes 3145728

commit v2 on v1

--- a/solution.py
+++ b/solution.py
@@ -18,7 +18,7 @@
     T, R, x_hbm, gain_hbm, nbias_hbm, w_hbm, cbias_hbm, out_ref,
     params, p_sem, xv, wv, hraw, eown, ehalo, own3, halo3, edge3, acc, stats,
     x_sem, w_sem, halo_send, halo_recv, eown_send, eown_recv,
-    ehalo_send, ehalo_recv, stat_send, stat_recv,
+    ehalo_send, ehalo_recv, stat_send, stat_recv, fwd_send, relayed, relay_sem,
 ):
     F, H, W, C = x_hbm.shape
     C3 = 3 * C
@@ -30,6 +30,12 @@
     def peer(offset):
         other = lax.rem(me + offset, n)
         return {"tm": other // R, "rows": lax.rem(other, R)}
+
+    def far(a, b):
+        return (a == T - 1) & (b == 0) & (T > 2)
+
+    def tm_of(d):
+        return lax.rem(me + n - d, n) // R
 
     x_copies = [pltpu.make_async_copy(x_hbm.at[f], xv.at[f], x_sem.at[f]) for f in range(F)]
     w_copies = [
@@ -45,7 +51,11 @@
     ]
     barrier = pltpu.get_barrier_semaphore()
     for d in range(1, n):
-        pl.semaphore_signal(barrier, inc=1, device_id=peer(d), device_id_type=MESH)
+        other = peer(d)
+
+        @pl.when(jnp.logical_not(far(tm, other["tm"])))
+        def _():
+            pl.semaphore_signal(barrier, inc=1, device_id=other, device_id_type=MESH)
     for c in x_copies + p_copies:
         c.start()
     def row_of(i):
@@ -60,6 +70,23 @@
             device_id={"tm": lax.rem(tm + 1, T), "rows": row},
             device_id_type=MESH,
         )
+
+    relay_in = pltpu.make_async_remote_copy(
+        src_ref=xv.at[pl.ds(F - 2, 2), pl.ds(H - 3, 1)],
+        dst_ref=relayed,
+        send_sem=relay_sem.at[0],
+        recv_sem=relay_sem.at[1],
+        device_id={"tm": T - 1, "rows": row},
+        device_id_type=MESH,
+    )
+    relay_out = pltpu.make_async_remote_copy(
+        src_ref=relayed,
+        dst_ref=hraw.at[:, pl.ds(H - 3, 1)],
+        send_sem=relay_sem.at[2],
+        recv_sem=halo_recv.at[H - 2],
+        device_id={"tm": max(T - 2, 0), "rows": row},
+        device_id_type=MESH,
+    )
 
     def last_copy(f):
         return pltpu.make_async_remote_copy(
@@ -96,25 +123,44 @@
         )
 
     has_next, has_prev = tm < T - 1, tm > 0
+    relays, relayed_by = (tm == T - 1) & (T == 4), (tm == T - 3) & (T == 4)
     sends_edge = (row < R - 1, row > 0)
     gets_edge = (row > 0, row < R - 1)
-
-    for c in w_copies:
-        c.start()
 
     total = jnp.zeros((8, C), jnp.float32)
     square = jnp.zeros((8, C), jnp.float32)
     for f in range(F):
-        x_copies[f].wait()
+        if f == 0:
+            x_copies[f].wait()
 
         def add_rows(r, carry):
             v = xv[f, r].astype(jnp.float32).reshape(W // 8, 8, C)
             return carry[0] + jnp.sum(v, axis=0), carry[1] + jnp.sum(v * v, axis=0)
 
         total, square = lax.fori_loop(0, H, add_rows, (total, square))
+        if f == 0:
+            for g in range(1, F):
+                x_copies[g].wait()
+            first = far(T - 1, tm)
+
+            @pl.when(first)
+            def _():
+                pl.semaphore_wait(barrier, n - 1 - R)
+
+            @pl.when(jnp.logical_not(first))
+            def _():
+                pl.semaphore_wait(barrier, n - 1)
+
+            @pl.when(has_next)
+            def _():
+                halo_copy(0, 0).start()
+
+            for c in w_copies:
+                c.start()
+
+
     stats[0, 0:1] = jnp.sum(total, axis=0, keepdims=True)
     stats[0, 1:2] = jnp.sum(square, axis=0, keepdims=True)
-    pl.semaphore_wait(barrier, n - 1)
 
     def stat_copy(d):
         return pltpu.make_async_remote_copy(
@@ -127,12 +173,23 @@
         )
 
     for d in range(1, n):
-        stat_copy(d).start()
+        @pl.when(jnp.logical_not(far(peer(d)["tm"], tm)))
+        def _():
+            stat_copy(d).start()
 
     @pl.when(has_next)
     def _():
-        for i in range(H - 1):
-            halo_copy(i, 0 if i == 0 else H - 1 if i == 1 else i - 1).start()
+        for i in range(1, H - 2):
+            halo_copy(i, H - 1 if i == 1 else i - 1).start()
+
+        @pl.when(relayed_by)
+        def _():
+            relay_in.start()
+
+        @pl.when(jnp.logical_not(relayed_by))
+        def _():
+            halo_copy(H - 2, H - 3).start()
+
         for f in (1, 0):
             last_copy(f).start()
 
@@ -140,6 +197,25 @@
         @pl.when(sends_edge[side])
         def _():
             own_edge(side).start()
+
+    def stat_forward(r):
+        d = (T - 1) * R + r - row
+        return pltpu.make_async_remote_copy(
+            src_ref=stats.at[R],
+            dst_ref=stats.at[d],
+            send_sem=fwd_send.at[r],
+            recv_sem=stat_recv.at[d],
+            device_id={"tm": T - 1, "rows": r},
+            device_id_type=MESH,
+        )
+
+    second = (tm == 1) & (T > 2)
+
+    @pl.when(second)
+    def _():
+        stat_copy(R).wait_recv()
+        for r in range(R):
+            stat_forward(r).start()
 
     for c in p_copies:
         c.wait()
@@ -150,7 +226,12 @@
 
         lax.fori_loop(0, H, start_acc, 0)
     for d in range(1, n):
-        stat_copy(d).wait_recv()
+        if d == R:
+            @pl.when(jnp.logical_not(second))
+            def _():
+                stat_copy(d).wait_recv()
+        else:
+            stat_copy(d).wait_recv()
     total = stats[0]
     for d in range(1, n):
         total = total + stats[d]
@@ -200,14 +281,10 @@
 
         lax.fori_loop(0, H, own_row, 0)
 
-    @pl.when(has_prev)
-    def _():
-        for i in range(2):
-            halo_copy(i, 0 if i == 0 else H - 1).wait_recv()
-        for side in range(2):
-            @pl.when(sends_edge[side])
-            def _():
-                halo_edge(side).start()
+    @pl.when(relays)
+    def _():
+        relay_in.wait_recv()
+        relay_out.start()
 
     for c in w_copies:
         c.wait()
@@ -237,6 +314,15 @@
 
     lax.fori_loop(0, H // OWN_ROWS, own_rows, 0)
 
+    @pl.when(has_prev)
+    def _():
+        for i in range(2):
+            halo_copy(i, 0 if i == 0 else H - 1).wait_recv()
+        for side in range(2):
+            @pl.when(sends_edge[side])
+            def _():
+                halo_edge(side).start()
+
     for side in range(2):
         kh = 0 if side == 0 else 2
         at = 1 if side == 0 else H
@@ -327,12 +413,32 @@
         lax.fori_loop(0, H, finish, 0)
 
     for d in range(1, n):
-        stat_copy(d).wait_send()
+        @pl.when(jnp.logical_not(far(peer(d)["tm"], tm)))
+        def _():
+            stat_copy(d).wait_send()
+
+    @pl.when(second)
+    def _():
+        for r in range(R):
+            stat_forward(r).wait_send()
+
+    @pl.when(relays)
+    def _():
+        relay_out.wait_send()
 
     @pl.when(has_next)
     def _():
-        for i in range(H - 1):
+        for i in range(H - 2):
             halo_copy(i, 0 if i == 0 else H - 1 if i == 1 else i - 1).wait_send()
+
+        @pl.when(relayed_by)
+        def _():
+            relay_in.wait_send()
+
+        @pl.when(jnp.logical_not(relayed_by))
+        def _():
+            halo_copy(H - 2, H - 3).wait_send()
+
         for f in (1, 0):
             last_copy(f).wait_send()
 
@@ -385,6 +491,9 @@
             dma((2,)),
             dma((n,)),
             dma((n,)),
+            dma((R,)),
+            pltpu.VMEM((2, 1, W, C), jnp.bfloat16),
+            dma((3,)),
         ],
         compiler_params=pltpu.CompilerParams(
             collective_id=0, has_side_effects=True, vmem_limit_bytes=50 * 1024 * 1024

time: 42.2 us -> 39.5 us (0.936)
  the two profiles are of different devices: /device:TPU:4 before, /device:TPU:10 now
where the time goes in v2:
time: 39.5 us; the launch traced here: 39.2 us
  Pallas kernels  38.1 us (96%)
  local copies, waits for them, and re-layouts  1.15 us (3%)
    pallas_call x1, Pallas kernels, shards(): pl.pallas_call(functools.partial(block_kernel, T, R), out_shape=jax.Shape...  38.1 us
    unnamed x1, local copies, waits for them, and re-layouts  1.15 us

profile of v2, /device:TPU:10, one launch (start us, length us, event | category | flops | bytes accessed | tf_op | source)
XLA Modules:
  0.0 39.2 jit_solution(15469821148206445491)
XLA Ops:
  0.0 38.1 %norm_conv_block.1 = bf16[2,8,128,384]{3,2,1,0:T(8,128)(2,1)S(1)} custom-call(bf16[2,8,128,384]{3,2,1,0:T(8,128)(2,1)} %bitcast.5, f32[384]{0:T(512)} %gain_hbm.1, f32[384]{0:T(512)} %nbias_hbm.1, bf16[3,3,1152,384]{3,2,1,0:T(8,128)(2,1)} %bitcast.4, f32[384]{0:T(512)} %cbias_hbm.1), custom_call_target="tpu_custom_call" | custom-call | tf_op jit(solution)/shard_map/norm_conv_block/pallas_call | solution.py:466
  38.1 1.1 %copy.7 = bf16[1,2,8,128,384]{4,3,2,1,0:T(8,128)(2,1)} copy(bf16[1,2,8,128,384]{4,3,2,1,0:T(8,128)(2,1)S(1)} %bitcast.3) | data formatting | bytes 3145728

commit v3 on v1

v3 whole, which is shorter than its diff:
```python
import functools

import jax
import jax.numpy as jnp
from jax import lax
from jax.experimental import pallas as pl
from jax.experimental.pallas import tpu as pltpu
from jax.sharding import PartitionSpec as P

GROUPS = 32
MESH = pl.DeviceIdType.MESH
OWN_ROWS = 4
LAST = 128

epsilon = 1e-06


def row_chunks(H):
    return [(0, 1), (H - 1, 1)] + [(r, min(2, H - 2 - r)) for r in range(1, H - 2, 2)]


def activated(raw, mean, half_scale, half_bias, put):
    W, _ = raw.shape
    column = lax.broadcasted_iota(jnp.int32, raw.shape, 0)
    h = (raw.astype(jnp.float32) - mean) * half_scale + half_bias
    a = h + h * jnp.tanh(h)
    put(0, jnp.where(column == 0, 0.0, pltpu.roll(a, 1, 0)).astype(jnp.bfloat16))
    put(1, a.astype(jnp.bfloat16))
    put(2, jnp.where(column == W - 1, 0.0, pltpu.roll(a, W - 1, 0)).astype(jnp.bfloat16))


def block_kernel(
    T, R, x_hbm, gain_hbm, nbias_hbm, w_hbm, cbias_hbm,
    out_ref, open_rows, hlast, norms, wlast,
    params, xv, wv, hraw, eown, ehalo, own3, halo3, edge3, acc, stats, relayed,
    p_sem, x_sem, w_sem, halo_send, halo_recv, edge_sem, stat_send, stat_recv, fwd_send, relay_sem,
):
    F, H, W, C = x_hbm.shape
    C3 = 3 * C
    n = T * R
    tm = lax.axis_index("tm")
    row = lax.axis_index("rows")
    me = tm * R + row

    def peer(offset):
        other = lax.rem(me + offset, n)
        return {"tm": other // R, "rows": lax.rem(other, R)}

    def landed(ref, sem):
        pltpu.make_async_copy(ref, ref, sem).wait()

    x_copies = [pltpu.make_async_copy(x_hbm.at[f], xv.at[f], x_sem.at[f]) for f in range(F)]
    w_copies = [
        pltpu.make_async_copy(w_hbm.at[kt, kh], wv.at[kt, :, pl.ds(kh * C, C)], w_sem.at[0])
        for kt in range(3)
        for kh in range(3)
    ]
    w_copies += [
        pltpu.make_async_copy(
            w_hbm.at[0, kh, pl.ds((kw + 1) * C - LAST, LAST)],
            wlast.at[pl.ds(kw * LAST, LAST), pl.ds(kh * C, C)],
            w_sem.at[1],
        )
        for kh in range(3)
        for kw in range(3)
    ]
    p_copies = [
        pltpu.make_async_copy(p, params.at[k, 0], p_sem.at[0])
        for k, p in enumerate((gain_hbm, nbias_hbm, cbias_hbm))
    ]

    def greets(other):
        return (other["tm"] > 0) | (tm == 0) | ((tm == 1) & (other["rows"] == row))

    def knows(other):
        return (tm > 0) | (other["tm"] == 0) | ((other["tm"] == 1) & (other["rows"] == row))

    barrier = pltpu.get_barrier_semaphore()
    for d in sorted(range(1, n), key=lambda d: abs(d - (n - R))):
        other = peer(d)

        @pl.when(greets(other))
        def _():
            pl.semaphore_signal(barrier, inc=1, device_id=other, device_id_type=MESH)

    for c in x_copies + p_copies:
        c.start()

    def row_of(i):
        return jnp.where(i == 0, 0, jnp.where(i == 1, H - 1, i - 1))

    chunks = row_chunks(H)
    nc = len(chunks)
    following = {"tm": lax.rem(tm + 1, T), "rows": row}

    def halo_copy(j):
        r, size = chunks[j]
        return pltpu.make_async_remote_copy(
            src_ref=xv.at[pl.ds(F - 2, 2), pl.ds(r, size)],
            dst_ref=hraw.at[:, pl.ds(r, size)],
            send_sem=halo_send.at[0],
            recv_sem=halo_recv.at[j],
            device_id=following,
            device_id_type=MESH,
        )

    def last_copy(k):
        src, dst = (
            (xv.at[F - 1, H - 2], hraw.at[1, H - 2]),
            (xv.at[F - 2, H - 2, :, : C - LAST], hraw.at[0, H - 2, :, : C - LAST]),
            (xv.at[F - 2, H - 2, :, C - LAST :], hlast),
        )[k]
        return pltpu.make_async_remote_copy(
            src_ref=src,
            dst_ref=dst,
            send_sem=halo_send.at[0],
            recv_sem=halo_recv.at[nc + k],
            device_id=following,
            device_id_type=MESH,
        )

    relay = nc - 2
    relay_row, relay_size = chunks[relay]
    relay_in = pltpu.make_async_remote_copy(
        src_ref=xv.at[pl.ds(F - 2, 2), pl.ds(relay_row, relay_size)],
        dst_ref=relayed,
        send_sem=halo_send.at[0],
        recv_sem=relay_sem.at[0],
        device_id={"tm": T - 1, "rows": row},
        device_id_type=MESH,
    )
    relay_out = pltpu.make_async_remote_copy(
        src_ref=relayed,
        dst_ref=hraw.at[:, pl.ds(relay_row, relay_size)],
        send_sem=relay_sem.at[1],
        recv_sem=halo_recv.at[relay],
        device_id={"tm": max(T - 2, 0), "rows": row},
        device_id_type=MESH,
    )

    def edge(side, src_ref, dst_ref, sem):
        s = side if R > 2 else 0
        target = row + 1 if side == 0 else row - 1
        return pltpu.make_async_remote_copy(
            src_ref=src_ref.at[:, pl.ds(H - 1 if side == 0 else 0, 1)],
            dst_ref=dst_ref.at[side],
            send_sem=edge_sem.at[sem, s],
            recv_sem=edge_sem.at[sem + 1, s],
            device_id={"tm": tm, "rows": lax.rem(target + R, R)},
            device_id_type=MESH,
        )

    def own_edge(side):
        return edge(side, xv, eown, 0)

    def halo_edge(side):
        return edge(side, hraw, ehalo, 2)

    has_next, has_prev = tm < T - 1, tm > 0
    relays, relayed_by = (tm == T - 1) & (T == 4), (tm == T - 3) & (T == 4)
    sends_edge = (row < R - 1, row > 0)
    gets_edge = (row > 0, row < R - 1)

    def add_rows(f, carry):
        def step(r, carry):
            v = xv[f, r].astype(jnp.float32).reshape(W // 8, 8, C)
            return carry[0] + jnp.sum(v, axis=0), carry[1] + jnp.sum(v * v, axis=0)

        return lax.fori_loop(0, H, step, carry)

    carry = (jnp.zeros((8, C), jnp.float32), jnp.zeros((8, C), jnp.float32))
    for f in range(F):
        x_copies[f].wait()
        carry = add_rows(f, carry)
    stats[0, 0:1] = jnp.sum(carry[0], axis=0, keepdims=True)
    stats[0, 1:2] = jnp.sum(carry[1], axis=0, keepdims=True)

    @pl.when(has_prev)
    def _():
        pl.semaphore_wait(barrier, n - 1)

    @pl.when(jnp.logical_not(has_prev))
    def _():
        pl.semaphore_wait(barrier, R if T > 1 else R - 1)

    def stat_copy(d):
        return pltpu.make_async_remote_copy(
            src_ref=stats.at[0],
            dst_ref=stats.at[d],
            send_sem=stat_send.at[0],
            recv_sem=stat_recv.at[1 if d == R else 0],
            device_id=peer(d),
            device_id_type=MESH,
        )

    for d in range(1, n):
        @pl.when(knows(peer(d)))
        def _():
            stat_copy(d).start()

    def stat_forward(t, r):
        d = t * R + r - row
        return pltpu.make_async_remote_copy(
            src_ref=stats.at[R],
            dst_ref=stats.at[d],
            send_sem=fwd_send.at[0],
            recv_sem=stat_recv.at[0],
            device_id={"tm": t, "rows": r},
            device_id_type=MESH,
        )

    def prev_stats():
        landed(stats.at[0], stat_recv.at[1])

    @pl.when(tm == 1)
    def _():
        prev_stats()
        for t in range(1, T):
            for r in range(R):
                if t == 1:
                    @pl.when(row != r)
                    def _():
                        stat_forward(t, r).start()
                else:
                    stat_forward(t, r).start()

    @pl.when(relayed_by)
    def _():
        relay_in.start()

    @pl.when(has_next)
    def _():
        halo_copy(0).start()

    for c in w_copies:
        c.start()

    for side in range(2):
        @pl.when(sends_edge[side])
        def _():
            own_edge(side).start()

    @pl.when(has_next)
    def _():
        for j in range(1, nc):
            if j == relay:
                @pl.when(jnp.logical_not(relayed_by))
                def _():
                    halo_copy(j).start()
            else:
                halo_copy(j).start()

        for k in range(3):
            last_copy(k).start()

    landed(params, p_sem.at[0])
    for f in range(F):
        def start_acc(r, _):
            acc[f, r + 1] = xv[f, r].astype(jnp.float32) + params[2]
            return 0

        lax.fori_loop(0, H, start_acc, 0)

    @pl.when(tm != 1)
    def _():
        prev_stats()

    landed(stats.at[pl.ds(0, n - 2)], stat_recv.at[0])
    total = stats[0]
    for d in range(1, n):
        total = total + stats[d]
    sums = jnp.concatenate(
        [jnp.broadcast_to(total[0:1], (8, C)), jnp.broadcast_to(total[1:2], (8, C))], axis=0
    )
    per_group = C // GROUPS
    channel = lax.broadcasted_iota(jnp.int32, (C, C), 0)
    other = lax.broadcasted_iota(jnp.int32, (C, C), 1)
    first = (other // per_group) * per_group
    member = jnp.where((channel >= first) & (channel < first + per_group), 1.0, 0.0)
    cells = 1.0 * F * H * W * per_group * n
    moments = (
        jnp.dot(
            sums,
            member.astype(jnp.float32),
            preferred_element_type=jnp.float32,
            precision=lax.Precision.HIGHEST,
        )
        / cells
    )
    mean = moments[0:1]
    var = jnp.maximum(moments[8:9] - mean * mean, 0.0)
    half_scale = lax.rsqrt(var + epsilon) * params[0] * 0.5
    half_bias = params[1] * 0.5
    norms[0:1] = mean
    norms[1:2] = half_scale
    norms[2:3] = half_bias

    def activate(raw, put):
        activated(raw, mean, half_scale, half_bias, put)

    for f in range(F):
        def own_row(r, _):
            def put(k, v):
                own3[f, r, :, k * C : (k + 1) * C] = v

            activate(xv[f, r], put)
            return 0

        lax.fori_loop(0, H, own_row, 0)

    landed(wv, w_sem.at[0])

    def product(lhs, kt, lo=0, hi=3):
        return jnp.dot(
            lhs, wv[kt, :, lo * C : hi * C], preferred_element_type=jnp.float32
        )

    def finish(r, _):
        for f in range(F):
            out_ref[f, r] = acc[f, r + 1].astype(out_ref.dtype)
        return 0

    def own_rows(g, _):
        r0 = g * OWN_ROWS

        @pl.when(relays & (g == H // OWN_ROWS // 2))
        def _():
            relay_in.wait_recv()
            relay_out.start()

        for kt in range(3):
            count = F - 2 + kt
            if count <= 0:
                continue
            lhs = own3[0:count, pl.ds(r0, OWN_ROWS)].reshape(count * OWN_ROWS * W, C3)
            y = product(lhs, kt)
            for kh in range(3):
                part = y[:, kh * C : (kh + 1) * C].reshape(count, OWN_ROWS, W, C)
                acc[2 - kt : 2 - kt + count, pl.ds(r0 + 2 - kh, OWN_ROWS)] += part
        return 0

    lax.fori_loop(0, H // OWN_ROWS, own_rows, 0)

    @pl.when(has_prev)
    def _():
        landed(stats.at[pl.ds(0, n - 1)], stat_send.at[0])

    @pl.when(jnp.logical_not(has_prev))
    def _():
        landed(stats.at[pl.ds(0, R if T > 1 else R - 1)], stat_send.at[0])

    @pl.when(tm == 1)
    def _():
        landed(stats.at[pl.ds(0, n - R - 1)], fwd_send.at[0])

    landed(wlast, w_sem.at[1])
    for side in range(2):
        @pl.when(sends_edge[side])
        def _():
            own_edge(side).wait_send()

    @pl.when(has_prev)
    def _():
        for j in range(2):
            halo_copy(j).wait_recv()
        for side in range(2):
            @pl.when(sends_edge[side])
            def _():
                halo_edge(side).start()

    for side in range(2):
        kh = 0 if side == 0 else 2
        at = 1 if side == 0 else H

        @pl.when(gets_edge[side])
        def _():
            own_edge(side).wait_recv()
            for f in range(F):
                def put(k, v):
                    edge3[f, :, k * C : (k + 1) * C] = v

                activate(eown[side, f, 0], put)
            for kt in range(3):
                count = F - 2 + kt
                if count > 0:
                    lhs = edge3[0:count].reshape(count * W, C3)
                    acc[2 - kt : 2 - kt + count, at] += product(lhs, kt, kh, kh + 1).reshape(
                        count, W, C
                    )

    @pl.when(has_prev)
    def _():
        def halo_row(i, _):
            r = row_of(i)

            for j in range(2, nc):
                @pl.when(r == chunks[j][0])
                def _():
                    halo_copy(j).wait_recv()

            for f in range(2):
                def put(k, v):
                    halo3[f, :, k * C : (k + 1) * C] = v

                activate(hraw[f, r], put)
            y = product(halo3[...].reshape(2 * W, C3), 0)
            z = product(halo3[1], 1)
            for kh in range(3):
                cols = slice(kh * C, (kh + 1) * C)
                acc[0, r + 2 - kh] += y[:W, cols] + z[:, cols]
                acc[1, r + 2 - kh] += y[W:, cols]

            @pl.when(i >= 2)
            def _():
                finish(i - 2, 0)

            return 0

        lax.fori_loop(0, 2, halo_row, 0)
        for side in range(2):
            kh = 0 if side == 0 else 2
            at = 1 if side == 0 else H

            @pl.when(gets_edge[side])
            def _():
                halo_edge(side).wait_recv()
                for f in range(2):
                    def put(k, v):
                        halo3[f, :, k * C : (k + 1) * C] = v

                    activate(ehalo[side, f, 0], put)
                y = product(halo3[...].reshape(2 * W, C3), 0, kh, kh + 1)
                z = product(halo3[1], 1, kh, kh + 1)
                acc[0, at] += y[:W] + z
                acc[1, at] += y[W:]

        lax.fori_loop(2, H - 1, halo_row, 0)

        for side in range(2):
            @pl.when(sends_edge[side])
            def _():
                halo_edge(side).wait_send()

        @pl.when(relays)
        def _():
            relay_out.wait_send()

        r = H - 2
        last_copy(0).wait_recv()

        def put(k, v):
            halo3[1, :, k * C : (k + 1) * C] = v

        activate(hraw[1, r], put)
        y = product(halo3[1], 0)
        z = product(halo3[1], 1)
        for kh in range(3):
            cols = slice(kh * C, (kh + 1) * C)
            acc[0, r + 2 - kh] += z[:, cols]
            out_ref[1, r + 1 - kh] = (acc[1, r + 2 - kh] + y[:, cols]).astype(out_ref.dtype)

        last_copy(1).wait_recv()
        part = C - LAST

        def put_part(k, v):
            halo3[0, :, k * part : (k + 1) * part] = v

        activated(
            hraw[0, r, :, :part], mean[:, :part], half_scale[:, :part], half_bias[:, :part], put_part
        )
        weights = jnp.concatenate([wv[0, kw * C : kw * C + part] for kw in range(3)], axis=0)
        y = jnp.dot(halo3[0, :, : 3 * part], weights, preferred_element_type=jnp.float32)
        for kh in range(3):
            open_rows[2 - kh] = acc[0, r + 2 - kh] + y[:, kh * C : (kh + 1) * C]
        last_copy(2).wait_recv()

    @pl.when(jnp.logical_not(has_prev))
    def _():
        lax.fori_loop(0, H, finish, 0)

    @pl.when(has_next)
    def _():
        landed(xv.at[pl.ds(F - 2, 2)], halo_send.at[0])


def tail_kernel(rows_ref, open_rows, hlast, norms, wlast, out_hbm, lhs, closed, sem):
    _, H, W, C = rows_ref.shape
    has_prev = lax.axis_index("tm") > 0
    ready = [
        pltpu.make_async_copy(rows_ref.at[1:], out_hbm.at[1:], sem.at[0]),
        pltpu.make_async_copy(
            rows_ref.at[0, pl.ds(0, H - 3)], out_hbm.at[0, pl.ds(0, H - 3)], sem.at[1]
        ),
    ]
    for c in ready:
        c.start()
    tops = pltpu.make_async_copy(
        rows_ref.at[0, pl.ds(H - 3, 3)], out_hbm.at[0, pl.ds(H - 3, 3)], sem.at[2]
    )
    lasts = pltpu.make_async_copy(closed, out_hbm.at[0, pl.ds(H - 3, 3)], sem.at[2])

    @pl.when(jnp.logical_not(has_prev))
    def _():
        tops.start()
        tops.wait()

    @pl.when(has_prev)
    def _():
        def put(k, v):
            lhs[:, k * LAST : (k + 1) * LAST] = v

        activated(
            hlast[...], norms[0:1, C - LAST :], norms[1:2, C - LAST :], norms[2:3, C - LAST :], put
        )
        y = jnp.dot(lhs[...], wlast[...], preferred_element_type=jnp.float32)
        for kh in range(3):
            closed[2 - kh] = (open_rows[2 - kh] + y[:, kh * C : (kh + 1) * C]).astype(closed.dtype)
        lasts.start()
        lasts.wait()

    for c in ready:
        c.wait()


def shards(T, R, inputs, norm_gain, norm_bias, conv_weight, conv_bias):
    _, F, H, W, C = inputs.shape
    n = T * R

    def pin(a):
        return pltpu.with_memory_space_constraint(a, pltpu.HBM)

    vmem = pl.BlockSpec(memory_space=pltpu.VMEM)
    hbm = pl.BlockSpec(memory_space=pltpu.HBM)
    anywhere = pl.BlockSpec(memory_space=pl.ANY)
    dma = pltpu.SemaphoreType.DMA
    parts = pl.pallas_call(
        functools.partial(block_kernel, T, R),
        out_shape=[
            jax.ShapeDtypeStruct((F, H, W, C), inputs.dtype),
            jax.ShapeDtypeStruct((3, W, C), jnp.float32),
            jax.ShapeDtypeStruct((W, LAST), inputs.dtype),
            jax.ShapeDtypeStruct((8, C), jnp.float32),
            jax.ShapeDtypeStruct((3 * LAST, 3 * C), conv_weight.dtype),
        ],
        in_specs=[hbm, anywhere, anywhere, hbm, anywhere],
        out_specs=[vmem] * 5,
        scratch_shapes=[
            pltpu.VMEM((3, 1, C), jnp.float32),
            pltpu.VMEM((F, H, W, C), jnp.bfloat16),
            pltpu.VMEM((3, 3 * C, 3 * C), jnp.bfloat16),
            pltpu.VMEM((2, H, W, C), jnp.bfloat16),
            pltpu.VMEM((2, F, 1, W, C), jnp.bfloat16),
            pltpu.VMEM((2, 2, 1, W, C), jnp.bfloat16),
            pltpu.VMEM((F, H, W, 3 * C), jnp.bfloat16),
            pltpu.VMEM((2, W, 3 * C), jnp.bfloat16),
            pltpu.VMEM((F, W, 3 * C), jnp.bfloat16),
            pltpu.VMEM((F, H + 2, W, C), jnp.float32),
            pltpu.VMEM((n, 2, C), jnp.float32),
            pltpu.VMEM((2, row_chunks(H)[-2][1], W, C), jnp.bfloat16),
            dma((1,)),
            dma((F,)),
            dma((2,)),
            dma((1,)),
            dma((len(row_chunks(H)) + 3,)),
            dma((4, 2 if R > 2 else 1)),
            dma((1,)),
            dma((2,)),
            dma((1,)),
            dma((2,)),
        ],
        compiler_params=pltpu.CompilerParams(
            collective_id=0, has_side_effects=True, vmem_limit_bytes=50 * 1024 * 1024
        ),
        name="norm_conv_block",
    )(
        pin(inputs.reshape(F, H, W, C)),
        pin(norm_gain),
        pin(norm_bias),
        pin(conv_weight.reshape(3, 3, 3 * C, C)),
        pin(conv_bias),
    )
    out = pl.pallas_call(
        tail_kernel,
        out_shape=jax.ShapeDtypeStruct((F, H, W, C), inputs.dtype),
        in_specs=[vmem] * 5,
        out_specs=hbm,
        scratch_shapes=[
            pltpu.VMEM((W, 3 * LAST), jnp.bfloat16),
            pltpu.VMEM((3, W, C), inputs.dtype),
            dma((3,)),
        ],
        compiler_params=pltpu.CompilerParams(vmem_limit_bytes=8 * 1024 * 1024),
        name="last_rows",
    )(*parts)
    return out.reshape(inputs.shape)


def solution(mesh):
    placed = (P("batch", "tm", "rows", None, None), P(), P(), P(), P())
    return jax.shard_map(
        functools.partial(shards, mesh.shape["tm"], mesh.shape["rows"]),
        mesh=mesh,
        in_specs=placed,
        out_specs=P("batch", "tm", "rows", None, None),
        check_vma=False,
    )
```

time: 42.2 us -> 38.6 us (0.915)
  the two profiles are of different devices: /device:TPU:4 before, /device:TPU:10 now
where the time goes in v3:
time: 38.6 us; the launch traced here: 38.3 us
  Pallas kernels  38.3 us (99%)
    pallas_call x1, Pallas kernels, shards(): pl.pallas_call(functools.partial(block_kernel, T, R), out_shape=[jax.Shap...  37.1 us
    pallas_call x1, Pallas kernels, shards(): pl.pallas_call(tail_kernel, out_shape=jax.ShapeDtypeStruct((F, H, W, C),...  1.17 us

profile of v3, /device:TPU:10, one launch (start us, length us, event | category | flops | bytes accessed | tf_op | source)
XLA Modules:
  0.0 38.3 jit_solution(17441173596424918335)
XLA Ops:
  0.0 37.1 %norm_conv_block.1 = (bf16[2,8,128,384]{3,2,1,0:T(8,128)(2,1)S(1)}, f32[3,128,384]{2,1,0:T(8,128)S(1)}, bf16[128,128]{1,0:T(8,128)(2,1)S(1)}, f32[8,384]{1,0:T(8,128)S(1)}, bf16[384,1152]{1,0:T(8,128)(2,1)S(1)}) custom-call(bf16[2,8,128,384]{3,2,1,0:T(8,128)(2,1)} %bitcast.4, f32[384]{0:T(512)} %gain_hbm.1, f32[384]{0:T(512)} %nbias_hbm.1, ...), custom_call_target="tpu_custom_call" | custom-call | tf_op jit(solution)/shard_map/norm_conv_block/pallas_call | solution.py:536
  37.1 1.2 %last_rows.1 = bf16[2,8,128,384]{3,2,1,0:T(8,128)(2,1)} custom-call(bf16[2,8,128,384]{3,2,1,0:T(8,128)(2,1)S(1)} %get-tuple-element.10.rows_ref, f32[3,128,384]{2,1,0:T(8,128)S(1)} %get-tuple-element.11.open_rows, bf16[128,128]{1,0:T(8,128)(2,1)S(1)} %get-tuple-element.12.hlast, f32[8,384]{1,0:T(8,128)S(1)} %get-tuple-element.13.norms, ...), custom_call_target="tpu_custom_call" | custom-call | tf_op jit(solution)/shard_map/last_rows/pallas_call | solution.py:582

commit v4 on v3

v4 whole, which is shorter than its diff:
```python
import functools

import jax
import jax.numpy as jnp
from jax import lax
from jax.experimental import pallas as pl
from jax.experimental.pallas import tpu as pltpu
from jax.sharding import PartitionSpec as P

GROUPS = 32
MESH = pl.DeviceIdType.MESH
OWN_ROWS = 4
LAST = 128

epsilon = 1e-06


def halo_chunks(H):
    half = (H - 1) // 2
    edges = [(1, 1, 0, 1), (0, 1, 0, 1), (0, 2, H - 1, 1)]
    newer = [(1, 1, 1, half), (1, 1, 1 + half, H - 2 - half)]
    older = [(0, 1, r, min(2, H - 2 - r)) for r in range(1, H - 2, 2)]
    return edges + newer + older


def activated(raw, mean, half_scale, half_bias, put):
    W, _ = raw.shape
    column = lax.broadcasted_iota(jnp.int32, raw.shape, 0)
    h = (raw.astype(jnp.float32) - mean) * half_scale + half_bias
    a = h + h * jnp.tanh(h)
    put(0, jnp.where(column == 0, 0.0, pltpu.roll(a, 1, 0)).astype(jnp.bfloat16))
    put(1, a.astype(jnp.bfloat16))
    put(2, jnp.where(column == W - 1, 0.0, pltpu.roll(a, W - 1, 0)).astype(jnp.bfloat16))


def block_kernel(
    T, R, x_hbm, gain_hbm, nbias_hbm, w_hbm, cbias_hbm,
    out_ref, open_rows, hlast, norms, wv,
    params, xv, hraw, eown, ehalo, own3, halo3, edge3, acc, stats, relayed, member,
    p_sem, x_sem, w_sem, halo_send, halo_recv, edge_sem, stat_send, stat_recv, relay_sem,
):
    F, H, W, C = x_hbm.shape
    C3 = 3 * C
    n = T * R
    tm = lax.axis_index("tm")
    row = lax.axis_index("rows")
    me = tm * R + row

    def peer(offset):
        other = lax.rem(me + offset, n)
        return {"tm": other // R, "rows": lax.rem(other, R)}

    def landed(ref, sem):
        pltpu.make_async_copy(ref, ref, sem).wait()

    x_copies = [pltpu.make_async_copy(x_hbm.at[f], xv.at[f], x_sem.at[0]) for f in range(F)]
    w_copies = [
        pltpu.make_async_copy(w_hbm.at[kt, kh], wv.at[kt, :, pl.ds(kh * C, C)], w_sem.at[0])
        for kt in range(3)
        for kh in range(3)
    ]
    p_copies = [
        pltpu.make_async_copy(p, params.at[k, 0], p_sem.at[0])
        for k, p in enumerate((gain_hbm, nbias_hbm, cbias_hbm))
    ]

    def lean(t):
        return (t == 0) | ((t == T - 2) & (T > 3))

    def waits(a, b):
        near = (a["tm"] == b["tm"]) | ((b["tm"] == a["tm"] + 1) & (a["rows"] == b["rows"]))
        return jnp.logical_not(lean(a["tm"])) | near

    mine = {"tm": tm, "rows": row}
    is_lean = lean(tm)
    passes_on = lean(tm - 1) & (tm > 0)
    met = R if T > 1 else R - 1

    def enter():
        @pl.when(is_lean)
        def _():
            pl.semaphore_wait(barrier, met)

        @pl.when(jnp.logical_not(is_lean))
        def _():
            pl.semaphore_wait(barrier, n - 1)

    barrier = pltpu.get_barrier_semaphore()
    for d in sorted(range(1, n), key=lambda d: abs(d - (n - R))):
        other = peer(d)

        @pl.when(waits(other, mine))
        def _():
            pl.semaphore_signal(barrier, inc=1, device_id=other, device_id_type=MESH)

        if d == n - R or n == R:
            for c in x_copies + p_copies:
                c.start()
            x_copies = p_copies = []
    for c in x_copies + p_copies:
        c.start()

    chunks = halo_chunks(H)
    nc = len(chunks)
    following = {"tm": lax.rem(tm + 1, T), "rows": row}

    def halo_copy(j):
        f, count, r, size = chunks[j]
        return pltpu.make_async_remote_copy(
            src_ref=xv.at[pl.ds(F - 2 + f, count), pl.ds(r, size)],
            dst_ref=hraw.at[pl.ds(f, count), pl.ds(r, size)],
            send_sem=halo_send.at[0],
            recv_sem=halo_recv.at[max(j - 2, 0)],
            device_id=following,
            device_id_type=MESH,
        )

    def first_half(k):
        half = pl.ds(k * (W // 2), W // 2)
        return pltpu.make_async_remote_copy(
            src_ref=xv.at[F - 1, 0, half],
            dst_ref=hraw.at[1, 0, half],
            send_sem=halo_send.at[0],
            recv_sem=halo_recv.at[0],
            device_id=following,
            device_id_type=MESH,
        )

    def last_copy(k):
        src, dst = (
            (xv.at[F - 2, H - 2, :, : C - LAST], hraw.at[0, H - 2, :, : C - LAST]),
            (xv.at[F - 2, H - 2, :, C - LAST :], hlast),
        )[k]
        return pltpu.make_async_remote_copy(
            src_ref=src,
            dst_ref=dst,
            send_sem=halo_send.at[0],
            recv_sem=halo_recv.at[nc - 2 + k],
            device_id=following,
            device_id_type=MESH,
        )

    relay = 4
    _, _, relay_row, relay_size = chunks[relay]
    relay_in = pltpu.make_async_remote_copy(
        src_ref=xv.at[pl.ds(F - 1, 1), pl.ds(relay_row, relay_size)],
        dst_ref=relayed,
        send_sem=halo_send.at[0],
        recv_sem=relay_sem.at[0],
        device_id={"tm": T - 1, "rows": row},
        device_id_type=MESH,
    )
    relay_out = pltpu.make_async_remote_copy(
        src_ref=relayed,
        dst_ref=hraw.at[pl.ds(1, 1), pl.ds(relay_row, relay_size)],
        send_sem=halo_send.at[0],
        recv_sem=halo_recv.at[relay - 2],
        device_id={"tm": max(T - 2, 0), "rows": row},
        device_id_type=MESH,
    )

    def edge(side, src_ref, dst_ref, sem):
        s = side if R > 2 else 0
        target = row + 1 if side == 0 else row - 1
        return pltpu.make_async_remote_copy(
            src_ref=src_ref.at[:, pl.ds(H - 1 if side == 0 else 0, 1)],
            dst_ref=dst_ref.at[side],
            send_sem=edge_sem.at[0, s],
            recv_sem=edge_sem.at[sem, s],
            device_id={"tm": tm, "rows": lax.rem(target + R, R)},
            device_id_type=MESH,
        )

    def own_edge(side):
        return edge(side, xv, eown, 1)

    def halo_edge(side):
        return edge(side, hraw, ehalo, 2)

    has_next, has_prev = tm < T - 1, tm > 0
    relays, relayed_by = (tm == T - 1) & (T == 4), (tm == T - 3) & (T == 4)
    sends_edge = (row < R - 1, row > 0)
    gets_edge = (row > 0, row < R - 1)

    def add_rows(f, carry):
        def step(r, carry):
            v = xv[f, r].astype(jnp.float32).reshape(W // 8, 8, C)
            return carry[0] + jnp.sum(v, axis=0), carry[1] + jnp.sum(v * v, axis=0)

        return lax.fori_loop(0, H, step, carry)

    early = is_lean & has_next
    carry = (jnp.zeros((8, C), jnp.float32), jnp.zeros((8, C), jnp.float32))
    landed(xv, x_sem.at[0])

    @pl.when(early & has_prev)
    def _():
        enter()
        first_half(0).start()

    carry = add_rows(0, carry)

    @pl.when(early & jnp.logical_not(has_prev))
    def _():
        enter()
        first_half(0).start()

    for f in range(1, F):
        carry = add_rows(f, carry)
    stats[0, 0:1] = jnp.sum(carry[0], axis=0, keepdims=True)
    stats[0, 1:2] = jnp.sum(carry[1], axis=0, keepdims=True)

    @pl.when(jnp.logical_not(early))
    def _():
        enter()

    def stat_copy(d):
        return pltpu.make_async_remote_copy(
            src_ref=stats.at[0],
            dst_ref=stats.at[d],
            send_sem=stat_send.at[0],
            recv_sem=stat_recv.at[1 if d == R else 0],
            device_id=peer(d),
            device_id_type=MESH,
        )

    for d in range(1, n):
        @pl.when(waits(mine, peer(d)))
        def _():
            stat_copy(d).start()

    def stat_forward(t, r):
        d = lax.rem((t + T + 1 - tm) * R + r - row + n, n)
        return pltpu.make_async_remote_copy(
            src_ref=stats.at[R],
            dst_ref=stats.at[d],
            send_sem=stat_send.at[0],
            recv_sem=stat_recv.at[0],
            device_id={"tm": t, "rows": r},
            device_id_type=MESH,
        )

    def prev_stats():
        landed(stats.at[0], stat_recv.at[1])

    @pl.when(has_next & jnp.logical_not(early))
    def _():
        first_half(0).start()

    @pl.when(passes_on)
    def _():
        prev_stats()
        for t in range(T):
            for r in range(R):
                @pl.when((tm != t + 1) & ((tm != t) | (row != r)))
                def _():
                    stat_forward(t, r).start()

    @pl.when(relayed_by)
    def _():
        relay_in.start()

    for c in w_copies:
        c.start()

    for side in range(2):
        @pl.when(sends_edge[side])
        def _():
            own_edge(side).start()

    @pl.when(has_next)
    def _():
        first_half(1).start()
        for j in range(1, nc):
            if j == relay:
                @pl.when(jnp.logical_not(relayed_by))
                def _():
                    halo_copy(j).start()
            else:
                halo_copy(j).start()

        for k in range(2):
            last_copy(k).start()

    landed(params, p_sem.at[0])
    per_group = C // GROUPS
    channel = lax.broadcasted_iota(jnp.int32, (C, C), 0)
    other = lax.broadcasted_iota(jnp.int32, (C, C), 1)
    first = (other // per_group) * per_group
    member[...] = jnp.where(
        (channel >= first) & (channel < first + per_group), 1.0, 0.0
    ).astype(jnp.bfloat16)
    for f in range(F):
        def start_acc(r, _):
            acc[f, r + 1] = xv[f, r].astype(jnp.float32) + params[2]
            return 0

        lax.fori_loop(0, H, start_acc, 0)

    @pl.when(jnp.logical_not(passes_on))
    def _():
        prev_stats()

    landed(stats.at[pl.ds(0, n - 2)], stat_recv.at[0])
    total = stats[0]
    for d in range(1, n):
        total = total + stats[d]
    high = total.astype(jnp.bfloat16)
    rest = total - high.astype(jnp.float32)
    middle = rest.astype(jnp.bfloat16)
    low = (rest - middle.astype(jnp.float32)).astype(jnp.bfloat16)
    pieces = [
        jnp.broadcast_to(p[k : k + 1], (16, C)) for k in range(2) for p in (high, middle, low)
    ]
    grouped = jnp.dot(
        jnp.concatenate(pieces, axis=0), member[...], preferred_element_type=jnp.float32
    )
    cells = 1.0 * F * H * W * per_group * n

    def moment(k):
        at = 48 * k
        three = grouped[at : at + 1] + grouped[at + 16 : at + 17] + grouped[at + 32 : at + 33]
        return three / cells

    moments = jnp.concatenate([moment(0), moment(1)], axis=0)
    mean = moments[0:1]
    var = jnp.maximum(moments[1:2] - mean * mean, 0.0)
    half_scale = lax.rsqrt(var + epsilon) * params[0] * 0.5
    half_bias = params[1] * 0.5
    norms[0:1] = mean
    norms[1:2] = half_scale
    norms[2:3] = half_bias

    def activate(raw, put):
        activated(raw, mean, half_scale, half_bias, put)

    for f in range(F):
        def own_row(r, _):
            def put(k, v):
                own3[f, r, :, k * C : (k + 1) * C] = v

            activate(xv[f, r], put)
            return 0

        lax.fori_loop(0, H, own_row, 0)

    landed(wv, w_sem.at[0])

    def product(lhs, kt, lo=0, hi=3):
        return jnp.dot(
            lhs, wv[kt, :, lo * C : hi * C], preferred_element_type=jnp.float32
        )

    def finish(r, _):
        for f in range(F):
            out_ref[f, r] = acc[f, r + 1].astype(out_ref.dtype)
        return 0

    def own_rows(g, _):
        r0 = g * OWN_ROWS

        @pl.when(relays & (g == H // OWN_ROWS // 2))
        def _():
            relay_in.wait_recv()
            relay_out.start()

        for kt in range(3):
            count = F - 2 + kt
            if count <= 0:
                continue
            lhs = own3[0:count, pl.ds(r0, OWN_ROWS)].reshape(count * OWN_ROWS * W, C3)
            y = product(lhs, kt)
            for kh in range(3):
                part = y[:, kh * C : (kh + 1) * C].reshape(count, OWN_ROWS, W, C)
                acc[2 - kt : 2 - kt + count, pl.ds(r0 + 2 - kh, OWN_ROWS)] += part
        return 0

    lax.fori_loop(0, H // OWN_ROWS, own_rows, 0)

    @pl.when(is_lean)
    def _():
        landed(stats.at[pl.ds(0, met)], stat_send.at[0])

    @pl.when(passes_on)
    def _():
        landed(stats.at[pl.ds(0, n - 1 + n - R - 1)], stat_send.at[0])

    @pl.when(jnp.logical_not(is_lean | passes_on))
    def _():
        landed(stats.at[pl.ds(0, n - 1)], stat_send.at[0])

    for side in range(2):
        @pl.when(sends_edge[side] & jnp.logical_not(has_prev))
        def _():
            own_edge(side).wait_send()

    @pl.when(has_prev)
    def _():
        landed(hraw.at[:, pl.ds(0, 2)], halo_recv.at[0])
        for side in range(2):
            @pl.when(sends_edge[side])
            def _():
                halo_edge(side).start()

    for side in range(2):
        kh = 0 if side == 0 else 2
        at = 1 if side == 0 else H

        @pl.when(gets_edge[side])
        def _():
            own_edge(side).wait_recv()
            for f in range(F):
                def put(k, v):
                    edge3[f, :, k * C : (k + 1) * C] = v

                activate(eown[side, f, 0], put)
            for kt in range(3):
                count = F - 2 + kt
                if count > 0:
                    lhs = edge3[0:count].reshape(count * W, C3)
                    acc[2 - kt : 2 - kt + count, at] += product(lhs, kt, kh, kh + 1).reshape(
                        count, W, C
                    )

    @pl.when(has_prev)
    def _():
        def halo_row(i, _):
            r = i * (H - 1)
            for f in range(2):
                def put(k, v):
                    halo3[f, :, k * C : (k + 1) * C] = v

                activate(hraw[f, r], put)
            y = product(halo3[...].reshape(2 * W, C3), 0)
            z = product(halo3[1], 1)
            for kh in range(3):
                cols = slice(kh * C, (kh + 1) * C)
                acc[0, r + 2 - kh] += y[:W, cols] + z[:, cols]
                acc[1, r + 2 - kh] += y[W:, cols]
            return 0

        def close(f, r):
            out_ref[f, r] = acc[f, r + 1].astype(out_ref.dtype)

        def arrive(f, r):
            for j in range(3, nc):
                if chunks[j][0] == f:
                    @pl.when(r == chunks[j][2])
                    def _():
                        halo_copy(j).wait_recv()

        def newer_row(r, _):
            arrive(1, r)

            def put(k, v):
                halo3[1, :, k * C : (k + 1) * C] = v

            activate(hraw[1, r], put)
            y = product(halo3[1], 0)
            z = product(halo3[1], 1)
            for kh in range(3):
                cols = slice(kh * C, (kh + 1) * C)
                acc[1, r + 2 - kh] += y[:, cols]
                acc[0, r + 2 - kh] += z[:, cols]
            close(1, r - 1)
            return 0

        def older_row(r, _):
            arrive(0, r)

            def put(k, v):
                halo3[0, :, k * C : (k + 1) * C] = v

            activate(hraw[0, r], put)
            y = product(halo3[0], 0)
            for kh in range(3):
                acc[0, r + 2 - kh] += y[:, kh * C : (kh + 1) * C]
            close(0, r - 1)
            return 0

        lax.fori_loop(0, 2, halo_row, 0)
        for side in range(2):
            kh = 0 if side == 0 else 2
            at = 1 if side == 0 else H

            @pl.when(gets_edge[side])
            def _():
                halo_edge(side).wait_recv()
                for f in range(2):
                    def put(k, v):
                        halo3[f, :, k * C : (k + 1) * C] = v

                    activate(ehalo[side, f, 0], put)
                y = product(halo3[...].reshape(2 * W, C3), 0, kh, kh + 1)
                z = product(halo3[1], 1, kh, kh + 1)
                acc[0, at] += y[:W] + z
                acc[1, at] += y[W:]

        lax.fori_loop(1, H - 1, newer_row, 0)
        for r in (H - 2, H - 1):
            close(1, r)

        for side in range(2):
            @pl.when(sends_edge[side])
            def _():
                s = side if R > 2 else 0
                landed(hraw.at[0, pl.ds(0, F + 2)], edge_sem.at[0, s])

        @pl.when(relays)
        def _():
            relay_out.wait_send()

        lax.fori_loop(1, H - 2, older_row, 0)

        r = H - 2
        last_copy(0).wait_recv()
        part = C - LAST

        def put_part(k, v):
            halo3[0, :, k * part : (k + 1) * part] = v

        activated(
            hraw[0, r, :, :part], mean[:, :part], half_scale[:, :part], half_bias[:, :part], put_part
        )
        weights = jnp.concatenate([wv[0, kw * C : kw * C + part] for kw in range(3)], axis=0)
        y = jnp.dot(halo3[0, :, : 3 * part], weights, preferred_element_type=jnp.float32)
        for kh in range(3):
            open_rows[2 - kh] = acc[0, r + 2 - kh] + y[:, kh * C : (kh + 1) * C]
        last_copy(1).wait_recv()

    @pl.when(jnp.logical_not(has_prev))
    def _():
        lax.fori_loop(0, H, finish, 0)

    @pl.when(has_next)
    def _():
        landed(xv.at[pl.ds(F - 2, 2)], halo_send.at[0])


def tail_kernel(F, rows_ref, open_rows, hlast, norms, wv, out_hbm, lhs, closed, sem):
    N, W, C = rows_ref.shape
    H = N // F
    has_prev = lax.axis_index("tm") > 0
    ready = [
        pltpu.make_async_copy(rows_ref.at[pl.ds(r, k)], out_hbm.at[pl.ds(r, k)], sem.at[0])
        for r, k in ((H, N - H), (0, H - 3))
        if k
    ]
    for c in ready:
        c.start()
    tops = pltpu.make_async_copy(
        rows_ref.at[pl.ds(H - 3, 3)], out_hbm.at[pl.ds(H - 3, 3)], sem.at[1]
    )
    lasts = pltpu.make_async_copy(closed, out_hbm.at[pl.ds(H - 3, 3)], sem.at[1])

    @pl.when(jnp.logical_not(has_prev))
    def _():
        tops.start()
        tops.wait()

    @pl.when(has_prev)
    def _():
        def put(k, v):
            lhs[:, k * LAST : (k + 1) * LAST] = v

        activated(
            hlast[...], norms[0:1, C - LAST :], norms[1:2, C - LAST :], norms[2:3, C - LAST :], put
        )
        weights = jnp.concatenate(
            [wv[0, (kw + 1) * C - LAST : (kw + 1) * C] for kw in range(3)], axis=0
        )
        y = jnp.dot(lhs[...], weights, preferred_element_type=jnp.float32)
        for kh in range(3):
            closed[2 - kh] = (open_rows[2 - kh] + y[:, kh * C : (kh + 1) * C]).astype(closed.dtype)
        lasts.start()
        lasts.wait()

    done = out_hbm.at[pl.ds(0, N - 3)]
    pltpu.make_async_copy(done, done, sem.at[0]).wait()


def shards(T, R, inputs, norm_gain, norm_bias, conv_weight, conv_bias):
    _, F, H, W, C = inputs.shape
    n = T * R

    def pin(a):
        return pltpu.with_memory_space_constraint(a, pltpu.HBM)

    vmem = pl.BlockSpec(memory_space=pltpu.VMEM)
    hbm = pl.BlockSpec(memory_space=pltpu.HBM)
    anywhere = pl.BlockSpec(memory_space=pl.ANY)
    dma = pltpu.SemaphoreType.DMA
    parts = pl.pallas_call(
        functools.partial(block_kernel, T, R),
        out_shape=[
            jax.ShapeDtypeStruct((F, H, W, C), inputs.dtype),
            jax.ShapeDtypeStruct((3, W, C), jnp.float32),
            jax.ShapeDtypeStruct((W, LAST), inputs.dtype),
            jax.ShapeDtypeStruct((8, C), jnp.float32),
            jax.ShapeDtypeStruct((3, 3 * C, 3 * C), conv_weight.dtype),
        ],
        in_specs=[hbm, anywhere, anywhere, hbm, anywhere],
        out_specs=[vmem] * 5,
        scratch_shapes=[
            pltpu.VMEM((3, 1, C), jnp.float32),
            pltpu.VMEM((F, H, W, C), jnp.bfloat16),
            pltpu.VMEM((2, H, W, C), jnp.bfloat16),
            pltpu.VMEM((2, F, 1, W, C), jnp.bfloat16),
            pltpu.VMEM((2, 2, 1, W, C), jnp.bfloat16),
            pltpu.VMEM((F, H, W, 3 * C), jnp.bfloat16),
            pltpu.VMEM((2, W, 3 * C), jnp.bfloat16),
            pltpu.VMEM((F, W, 3 * C), jnp.bfloat16),
            pltpu.VMEM((F, H + 2, W, C), jnp.float32),
            pltpu.VMEM((2 * n, 2, C), jnp.float32),
            pltpu.VMEM((1, halo_chunks(H)[4][3], W, C), jnp.bfloat16),
            pltpu.VMEM((C, C), jnp.bfloat16),
            dma((1,)),
            dma((1,)),
            dma((1,)),
            dma((1,)),
            dma((len(halo_chunks(H)),)),
            dma((3, 2 if R > 2 else 1)),
            dma((1,)),
            dma((2,)),
            dma((1,)),
        ],
        compiler_params=pltpu.CompilerParams(
            collective_id=0, has_side_effects=True, vmem_limit_bytes=36 * 1024 * 1024
        ),
        name="norm_conv_block",
    )(
        pin(inputs.reshape(F, H, W, C)),
        pin(norm_gain),
        pin(norm_bias),
        pin(conv_weight.reshape(3, 3, 3 * C, C)),
        pin(conv_bias),
    )
    out = pl.pallas_call(
        functools.partial(tail_kernel, F),
        out_shape=jax.ShapeDtypeStruct((F * H, W, C), inputs.dtype),
        in_specs=[vmem] * 5,
        out_specs=hbm,
        scratch_shapes=[
            pltpu.VMEM((W, 3 * LAST), jnp.bfloat16),
            pltpu.VMEM((3, W, C), inputs.dtype),
            dma((2,)),
        ],
        compiler_params=pltpu.CompilerParams(vmem_limit_bytes=4 * 1024 * 1024),
        name="last_rows",
    )(parts[0].reshape(F * H, W, C), *parts[1:])
    return out.reshape(inputs.shape)


def solution(mesh):
    placed = (P("batch", "tm", "rows", None, None), P(), P(), P(), P())
    return jax.shard_map(
        functools.partial(shards, mesh.shape["tm"], mesh.shape["rows"]),
        mesh=mesh,
        in_specs=placed,
        out_specs=P("batch", "tm", "rows", None, None),
        check_vma=False,
    )
```

time: 38.6 us -> 38.2 us (0.990)
  no operation moved by 1% of the time
where the time goes in v4:
time: 38.2 us; the launch traced here: 38.1 us
  Pallas kernels  38 us (99%)
    pallas_call x1, Pallas kernels, shards(): pl.pallas_call(functools.partial(block_kernel, T, R), out_shape=[jax.Shap...  36.9 us
    pallas_call x1, Pallas kernels, shards(): pl.pallas_call(functools.partial(tail_kernel, F), out_shape=jax.ShapeDtyp...  1.16 us

profile of v4, /device:TPU:10, one launch (start us, length us, event | category | flops | bytes accessed | tf_op | source)
XLA Modules:
  0.0 38.1 jit_solution(15400477515903631322)
XLA Ops:
  0.0 36.9 %norm_conv_block.1 = (bf16[2,8,128,384]{3,2,1,0:T(8,128)(2,1)S(1)}, f32[3,128,384]{2,1,0:T(8,128)S(1)}, bf16[128,128]{1,0:T(8,128)(2,1)S(1)}, f32[8,384]{1,0:T(8,128)S(1)}, bf16[3,1152,1152]{2,1,0:T(8,128)(2,1)S(1)}) custom-call(bf16[2,8,128,384]{3,2,1,0:T(8,128)(2,1)} %bitcast.6, f32[384]{0:T(512)} %gain_hbm.1, f32[384]{0:T(512)} %nbias_hbm.1, ...), custom_call_target="tpu_custom_call" | custom-call | tf_op jit(solution)/shard_map/norm_conv_block/pallas_call | solution.py:593
  36.9 1.2 %last_rows.1 = bf16[16,128,384]{2,1,0:T(8,128)(2,1)} custom-call(bf16[16,128,384]{2,1,0:T(8,128)(2,1)S(1)} %bitcast.4, f32[3,128,384]{2,1,0:T(8,128)S(1)} %get-tuple-element.11.open_rows, bf16[128,128]{1,0:T(8,128)(2,1)S(1)} %get-tuple-element.12.hlast, f32[8,384]{1,0:T(8,128)S(1)} %get-tuple-element.13.norms, bf16[3,1152,1152]{2,1,0:T(8,128)(2,1)S(1)} %get-tuple-element.14.wv), custom_call_target="tpu_custom_call" | custom-call | tf_op jit(solution)/shard_map/last_rows/pallas_call | solution.py:638

commit v5 on v4

--- a/solution.py
+++ b/solution.py
@@ -193,17 +193,12 @@
     carry = (jnp.zeros((8, C), jnp.float32), jnp.zeros((8, C), jnp.float32))
     landed(xv, x_sem.at[0])
 
-    @pl.when(early & has_prev)
+    @pl.when(early)
     def _():
         enter()
         first_half(0).start()
 
     carry = add_rows(0, carry)
-
-    @pl.when(early & jnp.logical_not(has_prev))
-    def _():
-        enter()
-        first_half(0).start()
 
     for f in range(1, F):
         carry = add_rows(f, carry)
@@ -260,14 +255,6 @@
     def _():
         relay_in.start()
 
-    for c in w_copies:
-        c.start()
-
-    for side in range(2):
-        @pl.when(sends_edge[side])
-        def _():
-            own_edge(side).start()
-
     @pl.when(has_next)
     def _():
         first_half(1).start()
@@ -281,6 +268,14 @@
 
         for k in range(2):
             last_copy(k).start()
+
+    for side in range(2):
+        @pl.when(sends_edge[side])
+        def _():
+            own_edge(side).start()
+
+    for c in w_copies:
+        c.start()
 
     landed(params, p_sem.at[0])
     per_group = C // GROUPS

time: 38.2 us -> 38.2 us (level)
  no operation moved by 1% of the time
where the time goes in v5:
time: 38.2 us; the launch traced here: 37.8 us
  Pallas kernels  37.8 us (99%)
    pallas_call x1, Pallas kernels, shards(): pl.pallas_call(functools.partial(block_kernel, T, R), out_shape=[jax.Shap...  36.7 us
    pallas_call x1, Pallas kernels, shards(): pl.pallas_call(functools.partial(tail_kernel, F), out_shape=jax.ShapeDtyp...  1.16 us

profile of v5, /device:TPU:10, one launch (start us, length us, event | category | flops | bytes accessed | tf_op | source)
XLA Modules:
  0.0 37.8 jit_solution(14592813613161224997)
XLA Ops:
  0.0 36.7 %norm_conv_block.1 = (bf16[2,8,128,384]{3,2,1,0:T(8,128)(2,1)S(1)}, f32[3,128,384]{2,1,0:T(8,128)S(1)}, bf16[128,128]{1,0:T(8,128)(2,1)S(1)}, f32[8,384]{1,0:T(8,128)S(1)}, bf16[3,1152,1152]{2,1,0:T(8,128)(2,1)S(1)}) custom-call(bf16[2,8,128,384]{3,2,1,0:T(8,128)(2,1)} %bitcast.6, f32[384]{0:T(512)} %gain_hbm.1, f32[384]{0:T(512)} %nbias_hbm.1, ...), custom_call_target="tpu_custom_call" | custom-call | tf_op jit(solution)/shard_map/norm_conv_block/pallas_call | solution.py:588
  36.7 1.2 %last_rows.1 = bf16[16,128,384]{2,1,0:T(8,128)(2,1)} custom-call(bf16[16,128,384]{2,1,0:T(8,128)(2,1)S(1)} %bitcast.4, f32[3,128,384]{2,1,0:T(8,128)S(1)} %get-tuple-element.11.open_rows, bf16[128,128]{1,0:T(8,128)(2,1)S(1)} %get-tuple-element.12.hlast, f32[8,384]{1,0:T(8,128)S(1)} %get-tuple-element.13.norms, bf16[3,1152,1152]{2,1,0:T(8,128)(2,1)S(1)} %get-tuple-element.14.wv), custom_call_target="tpu_custom_call" | custom-call | tf_op jit(solution)/shard_map/last_rows/pallas_call | solution.py:633

commit v6 on v5

--- a/solution.py
+++ b/solution.py
@@ -115,11 +115,12 @@
             device_id_type=MESH,
         )
 
-    def first_half(k):
-        half = pl.ds(k * (W // 2), W // 2)
+    def first_row(k):
+        cut = 3 * W // 4
+        part = pl.ds(0, cut) if k == 0 else pl.ds(cut, W - cut)
         return pltpu.make_async_remote_copy(
-            src_ref=xv.at[F - 1, 0, half],
-            dst_ref=hraw.at[1, 0, half],
+            src_ref=xv.at[F - 1, 0, part],
+            dst_ref=hraw.at[1, 0, part],
             send_sem=halo_send.at[0],
             recv_sem=halo_recv.at[0],
             device_id=following,
@@ -196,7 +197,7 @@
     @pl.when(early)
     def _():
         enter()
-        first_half(0).start()
+        first_row(0).start()
 
     carry = add_rows(0, carry)
 
@@ -240,7 +241,7 @@
 
     @pl.when(has_next & jnp.logical_not(early))
     def _():
-        first_half(0).start()
+        first_row(0).start()
 
     @pl.when(passes_on)
     def _():
@@ -257,7 +258,7 @@
 
     @pl.when(has_next)
     def _():
-        first_half(1).start()
+        first_row(1).start()
         for j in range(1, nc):
             if j == relay:
                 @pl.when(jnp.logical_not(relayed_by))

time: 38.2 us -> 38.2 us (level)
  no operation moved by 1% of the time
where the time goes in v6:
time: 38.2 us; the launch traced here: 37.8 us
  Pallas kernels  37.8 us (99%)
    pallas_call x1, Pallas kernels, shards(): pl.pallas_call(functools.partial(block_kernel, T, R), out_shape=[jax.Shap...  36.7 us
    pallas_call x1, Pallas kernels, shards(): pl.pallas_call(functools.partial(tail_kernel, F), out_shape=jax.ShapeDtyp...  1.16 us

profile of v6, /device:TPU:10, one launch (start us, length us, event | category | flops | bytes accessed | tf_op | source)
XLA Modules:
  0.0 37.8 jit_solution(4375775620030441810)
XLA Ops:
  0.0 36.7 %norm_conv_block.1 = (bf16[2,8,128,384]{3,2,1,0:T(8,128)(2,1)S(1)}, f32[3,128,384]{2,1,0:T(8,128)S(1)}, bf16[128,128]{1,0:T(8,128)(2,1)S(1)}, f32[8,384]{1,0:T(8,128)S(1)}, bf16[3,1152,1152]{2,1,0:T(8,128)(2,1)S(1)}) custom-call(bf16[2,8,128,384]{3,2,1,0:T(8,128)(2,1)} %bitcast.6, f32[384]{0:T(512)} %gain_hbm.1, f32[384]{0:T(512)} %nbias_hbm.1, ...), custom_call_target="tpu_custom_call" | custom-call | tf_op jit(solution)/shard_map/norm_conv_block/pallas_call | solution.py:589
  36.7 1.2 %last_rows.1 = bf16[16,128,384]{2,1,0:T(8,128)(2,1)} custom-call(bf16[16,128,384]{2,1,0:T(8,128)(2,1)S(1)} %bitcast.4, f32[3,128,384]{2,1,0:T(8,128)S(1)} %get-tuple-element.11.open_rows, bf16[128,128]{1,0:T(8,128)(2,1)S(1)} %get-tuple-element.12.hlast, f32[8,384]{1,0:T(8,128)S(1)} %get-tuple-element.13.norms, bf16[3,1152,1152]{2,1,0:T(8,128)(2,1)S(1)} %get-tuple-element.14.wv), custom_call_target="tpu_custom_call" | custom-call | tf_op jit(solution)/shard_map/last_rows/pallas_call | solution.py:634
